TPU v7x, 32 devices: a whole 2x2x4 slice. The times are simulated.
32 devices in a mesh: ctx: 8 (over z, y), head: 4 (over x, core).
Axes of the slice: x: 2, y: 2, z: 4, core: 2. Of those that a mesh axis runs over, the one named last changes fastest.
Arguments:
- query_input: bfloat16 [4096, 4096], P(('ctx', 'head')), may hold values from -6 to 6
- key_input: bfloat16 [4096, 4096], P(('ctx', 'head')), may hold values from -6 to 6
- value_input: bfloat16 [4096, 4096], P(('ctx', 'head')), may hold values from -6 to 6
- cotangent: bfloat16 [4096, 4096], P(('ctx', 'head')), may hold values from -6 to 6
- level_codes: int32 [32, 13, 4096], P('head', None, 'ctx'), may hold values from 0 to 15
Outputs:
- attended: bfloat16 [4096, 4096], P(('ctx', 'head'))
- grad_queries: bfloat16 [4096, 4096], P(('ctx', 'head'))
- grad_keys: bfloat16 [4096, 4096], P(('ctx', 'head'))
- grad_values: bfloat16 [4096, 4096], P(('ctx', 'head'))
All inputs are finite; a program needn't handle non-finite values.
Results may differ from a plain program's by a relative error of at most 0.0074.
Values may be sent and summed in bfloat16 or wider, within the bound.
No kernel may reach another device: no remote copies, remote signals or barrier semaphores. Data moves between devices by JAX's collectives and lax.ppermute only.
A program may use at most 128 MiB of HBM per device.

v0:
```python
import jax
import jax.numpy as jnp
from jax import lax
from jax.sharding import PartitionSpec as P


def swapped(block, axis, stride):
    count = lax.axis_size(axis)
    route = []
    for low in range(count):
        high = low | 1 << stride
        if high != low and high < count:
            route += [(low, high), (high, low)]
    return lax.ppermute(block, axis, route)


def level_gain(level):
    if level == 0:
        return 1.0
    return 2.0 ** (-(level - 1) / 2.0)


def member_of(owner_block, member_block, bit_index):
    bit_span = 2**bit_index
    owner_set = owner_block // bit_span % 2 == 1
    member_clear = member_block // bit_span % 2 == 0
    same_parent = owner_block // (2 * bit_span) == member_block // (2 * bit_span)
    return jnp.where(owner_set & member_clear & same_parent, 1.0, 0.0).astype(jnp.float32)


def on_device(query_input, key_input, value_input, cotangent, level_codes):
    query_rows, key_rows, value_rows, cot_rows = (
        lax.all_to_all(query_input, "head", split_axis=1, concat_axis=0, tiled=True),
        lax.all_to_all(key_input, "head", split_axis=1, concat_axis=0, tiled=True),
        lax.all_to_all(value_input, "head", split_axis=1, concat_axis=0, tiled=True),
        lax.all_to_all(cotangent, "head", split_axis=1, concat_axis=0, tiled=True),
    )
    head_count = level_codes.shape[0]
    total_levels = level_codes.shape[1]
    length = query_rows.shape[0]
    head_dim = query_rows.shape[1] // head_count
    tok_bits = length.bit_length() - 1
    ctx_bits = total_levels - tok_bits - 1
    score_scale = head_dim ** (-0.5)
    head_shape = (length, head_count, head_dim)
    query_heads = query_rows.reshape(head_shape)
    key_heads = key_rows.reshape(head_shape)
    value_heads = value_rows.reshape(head_shape)
    cot_heads = cot_rows.reshape(head_shape)
    code_weights = level_codes.astype(jnp.float32) / 8.0
    my_block = lax.axis_index("ctx")
    cross_scale = jnp.stack(
        [
            code_weights[:, tok_bits + 1 + bit_index, :]
            * (score_scale * level_gain(tok_bits + 1 + bit_index))
            * (my_block // 2**bit_index % 2).astype(jnp.float32)
            for bit_index in range(ctx_bits)
        ]
    )
    row_scale = jnp.transpose(cross_scale, (0, 2, 1))
    block_state = jnp.einsum(
        "phd,phe->hde", key_heads, value_heads, preferred_element_type=jnp.float32
    )
    scaled_cot = (row_scale[..., None] * cot_heads[None]).astype(jnp.bfloat16)
    grad_state = jnp.einsum(
        "phd,bphe->bhde", query_heads, scaled_cot, preferred_element_type=jnp.float32
    )
    running = block_state
    bucket_list = []
    for bit_index in range(ctx_bits):
        partner = swapped(running, "ctx", bit_index)
        bit_set = (my_block // 2**bit_index % 2).astype(jnp.float32)
        bucket_list.append(bit_set * partner)
        running = running + partner
    bucket_sums = jnp.stack(bucket_list)
    bucket = bucket_sums.astype(jnp.bfloat16)
    term_rows = head_count * head_dim
    targets = jnp.arange(term_rows * lax.axis_size("ctx") // term_rows, dtype=jnp.int32)
    chosen = jnp.stack(
        [member_of(my_block, targets, bit_index) for bit_index in range(ctx_bits)], axis=1
    )
    spread = jnp.einsum("tb,bhde->thde", chosen, grad_state, precision=lax.Precision.HIGHEST)
    pulled = lax.psum_scatter(
        spread.reshape(term_rows * lax.axis_size("ctx"), head_dim),
        "ctx",
        scatter_dimension=0,
        tiled=True,
    ).reshape(head_count, head_dim, head_dim)
    pulled_half = pulled.astype(jnp.bfloat16)
    block_rows = min(512, length)
    steps_count = length // block_rows
    places = jnp.arange(length, dtype=jnp.int32)

    def row_step(carried_grads, block_index):
        key_grad, value_grad = carried_grads
        first_row = block_index * block_rows
        rows_at = first_row + jnp.arange(block_rows, dtype=jnp.int32)
        levels = jnp.zeros((block_rows, length), jnp.int32)
        for bit_index in range(tok_bits):
            levels = levels + (
                rows_at[:, None] // 2**bit_index != places[None, :] // 2**bit_index
            ).astype(jnp.int32)
        weight = jnp.zeros((head_count, block_rows, length), jnp.float32)
        for level_index in range(tok_bits + 1):
            weight = jnp.where(
                (levels == level_index)[None],
                code_weights[:, level_index, :, None] * level_gain(level_index),
                weight,
            )
        weight = jnp.where((places[None, :] <= rows_at[:, None])[None], weight, 0.0)
        scores = jnp.einsum(
            "phd,shd->hps", query_heads, key_heads, preferred_element_type=jnp.float32
        )
        attention = (score_scale * weight * scores).astype(jnp.bfloat16)
        local_out = jnp.einsum(
            "hps,she->phe", attention, value_heads, preferred_element_type=jnp.float32
        )
        dots = jnp.einsum(
            "phe,she->hps", cot_heads, value_heads, preferred_element_type=jnp.float32
        )
        score_grads = (score_scale * weight * dots).astype(jnp.bfloat16)
        local_qgrad = jnp.einsum(
            "hps,shd->phd", score_grads, key_heads, preferred_element_type=jnp.float32
        )
        key_grad = key_grad + jnp.einsum(
            "hps,phd->shd", score_grads, query_heads, preferred_element_type=jnp.float32
        )
        value_grad = value_grad + jnp.einsum(
            "hps,phe->she", attention, cot_heads, preferred_element_type=jnp.float32
        )
        return ((key_grad, value_grad), (local_out, local_qgrad))

    zero_grads = jnp.zeros(head_shape, jnp.float32)
    (key_local, value_local), (local_out, local_qgrad) = lax.scan(
        row_step, (zero_grads, zero_grads), jnp.arange(steps_count, dtype=jnp.int32)
    )
    local_out = local_out.reshape(head_shape)
    local_qgrad = local_qgrad.reshape(head_shape)
    cross_out = jnp.sum(
        row_scale[..., None]
        * jnp.einsum("phd,bhde->bphe", query_heads, bucket, preferred_element_type=jnp.float32),
        axis=0,
    )
    cross_qgrad = jnp.sum(
        row_scale[..., None]
        * jnp.einsum("phe,bhde->bphd", cot_heads, bucket, preferred_element_type=jnp.float32),
        axis=0,
    )
    flat_shape = (length, head_count * head_dim)
    attended = (local_out + cross_out).astype(jnp.bfloat16).reshape(flat_shape)
    grad_query = (local_qgrad + cross_qgrad).astype(jnp.bfloat16).reshape(flat_shape)
    grad_key = (
        (
            key_local
            + jnp.einsum(
                "phe,hde->phd", value_heads, pulled_half, preferred_element_type=jnp.float32
            )
        )
        .astype(jnp.bfloat16)
        .reshape(flat_shape)
    )
    grad_value = (
        (
            value_local
            + jnp.einsum("phd,hde->phe", key_heads, pulled_half, preferred_element_type=jnp.float32)
        )
        .astype(jnp.bfloat16)
        .reshape(flat_shape)
    )
    return (
        lax.all_to_all(attended, "head", split_axis=0, concat_axis=1, tiled=True),
        lax.all_to_all(grad_query, "head", split_axis=0, concat_axis=1, tiled=True),
        lax.all_to_all(grad_key, "head", split_axis=0, concat_axis=1, tiled=True),
        lax.all_to_all(grad_value, "head", split_axis=0, concat_axis=1, tiled=True),
    )


def solution(mesh):
    return jax.shard_map(
        on_device,
        mesh=mesh,
        in_specs=(
            P(("ctx", "head"), None),
            P(("ctx", "head"), None),
            P(("ctx", "head"), None),
            P(("ctx", "head"), None),
            P("head", None, "ctx"),
        ),
        out_specs=(
            P(("ctx", "head"), None),
            P(("ctx", "head"), None),
            P(("ctx", "head"), None),
            P(("ctx", "head"), None),
        ),
        check_vma=False,
    )
```

profile of v0, /device:TPU:0, one launch (start us, length us, event | category | flops | bytes accessed | tf_op | source)
XLA Modules:
  0.0 264.9 jit_solution(6928649475833172917)
XLA Ops:
  7.2 2.4 copy.203
  9.5 4.4 %all-to-all-start = ((bf16[128,4,1024]{2,0,1:T(8,128)(2,1)}), bf16[128,4,1024]{2,0,1:T(8,128)(2,1)S(1)}, u32[]{:S(2)}, u32[]{:S(2)}) async-start(bf16[128,4,1024]{2,0,1:T(8,128)(2,1)} %bitcast.123), calls=%async_computation | async-start | bytes 2097152 | tf_op jit(solution)/shard_map/all_to_all | solution.py:33
  13.9 1.1 copy.200
  15.0 13.4 %all-to-all-done = bf16[128,4,1024]{2,0,1:T(8,128)(2,1)S(1)} async-done(((bf16[128,4,1024]{2,0,1:T(8,128)(2,1)}), bf16[128,4,1024]{2,0,1:T(8,128)(2,1)S(1)}, u32[]{:S(2)}, u32[]{:S(2)}) %all-to-all-start) | async-done | bytes 1048608 | tf_op jit(solution)/shard_map/all_to_all | solution.py:33
  28.3 3.5 %all-to-all-start.4 = ((bf16[128,4,1024]{2,0,1:T(8,128)(2,1)}), bf16[128,4,1024]{2,0,1:T(8,128)(2,1)S(1)}, u32[]{:S(2)}, u32[]{:S(2)}) async-start(bf16[128,4,1024]{2,0,1:T(8,128)(2,1)} %bitcast.120), calls=%async_computation.4 | async-start | bytes 2097152 | tf_op jit(solution)/shard_map/all_to_all | solution.py:36
  31.9 1.0 convert_multiply_fusion
  33.6 1.1 copy.202
  34.7 1.2 copy.158
  36.0 10.3 %all-to-all-done.4 = bf16[128,4,1024]{2,0,1:T(8,128)(2,1)S(1)} async-done(((bf16[128,4,1024]{2,0,1:T(8,128)(2,1)}), bf16[128,4,1024]{2,0,1:T(8,128)(2,1)S(1)}, u32[]{:S(2)}, u32[]{:S(2)}) %all-to-all-start.4) | async-done | bytes 1048608 | tf_op jit(solution)/shard_map/all_to_all | solution.py:36
  46.3 4.3 %all-to-all-start.1 = ((bf16[128,4,1024]{2,0,1:T(8,128)(2,1)}), bf16[128,4,1024]{2,0,1:T(8,128)(2,1)}, u32[]{:S(2)}, u32[]{:S(2)}) async-start(bf16[128,4,1024]{2,0,1:T(8,128)(2,1)} %bitcast.122), calls=%async_computation.1 | async-start | bytes 2097152 | tf_op jit(solution)/shard_map/all_to_all | solution.py:34
  51.1 1.9 copy.118
  53.0 4.0 %fusion.9 = f32[3,8,128,128]{2,3,0,1:T(8,128)} fusion(f32[512,8,128]{0,2,1:T(8,128)} %copy.118, f32[3,512,8]{1,0,2:T(4,128)S(1)} %copy.99, bf16[512,8,128,1]{2,1,0,3:T(8,128)(2,1)} %bitcast.136), kind=kOutput, calls=%fused_computation.19 | convolution fusion | flops 405798912 | bytes 4767744 | tf_op jit(solution)/shard_map/phd,bphe->bhde/dot_general | solution.py:65
  57.0 2.0 copy.120
  59.0 4.4 %fusion.53 = f32[8,8,128,128]{3,0,2,1:T(8,128)S(1)} fusion(f32[3,8,128,128]{3,0,2,1:T(4,128)S(1)} %copy.120, f32[8,1]{0,1:T(1,128)S(1)} %and_select_fusion, f32[8,1]{0,1:T(1,128)S(1)} %and_select_fusion.3, f32[8,1]{0,1:T(1,128)S(1)} %and_select_fusion.6), kind=kOutput, calls=%fused_computation.129 | convolution fusion | flops 37748784 | bytes 5767264 | tf_op jit(solution)/shard_map/tb,bhde->thde/dot_general | solution.py:82
  63.4 2.7 %copy.121 = f32[8,8,128,128]{3,2,1,0:T(8,128)} copy(f32[8,8,128,128]{3,0,2,1:T(8,128)S(1)} %fusion.53) | data formatting | bytes 8388608 | tf_op jit(solution)/shard_map/tb,bhde->thde/dot_general | solution.py:82
  66.2 1.2 copy-done.4
  67.4 1.1 copy.201
  68.4 3.7 %all-to-all-start.2 = ((bf16[128,4,1024]{2,0,1:T(8,128)(2,1)}), bf16[128,4,1024]{2,0,1:T(8,128)(2,1)S(1)}, u32[]{:S(2)}, u32[]{:S(2)}) async-start(bf16[128,4,1024]{2,0,1:T(8,128)(2,1)} %bitcast.121), calls=%async_computation.2 | async-start | bytes 2097152 | tf_op jit(solution)/shard_map/all_to_all | solution.py:35
  72.3 1.5 copy.159
  73.8 12.7 %all-to-all-done.2 = bf16[128,4,1024]{2,0,1:T(8,128)(2,1)S(1)} async-done(((bf16[128,4,1024]{2,0,1:T(8,128)(2,1)}), bf16[128,4,1024]{2,0,1:T(8,128)(2,1)S(1)}, u32[]{:S(2)}, u32[]{:S(2)}) %all-to-all-start.2) | async-done | bytes 1048608 | tf_op jit(solution)/shard_map/all_to_all | solution.py:35
  86.4 1.0 copy-done.1
  87.4 1.5 copy.160
  89.6 2.3 collective-permute-start
  91.9 3.0 %broadcast_compare_fusion.9 = (pred[512,512]{1,0:T(8,128)(4,1)S(1)}, pred[512,512]{1,0:T(8,128)(4,1)S(1)}, pred[512,512]{1,0:T(8,128)(4,1)S(1)}, pred[512,512]{1...) fusion(s32[512]{0:T(512)S(1)} %get-tuple-element.72, ...), kind=kLoop, calls=%fused_computation.60 | loop fusion | flops 9437184 | bytes 2637824 | tf_op jit(solution)/shard_map/while/body/eval_jaxpr/eq | solution.py:106
  94.9 14.3 %collective-permute-done = f32[8,128,128]{2,1,0:T(8,128)S(1)} collective-permute-done((f32[8,128,128]{2,1,0:T(8,128)S(1)}, f32[8,128,128]{2,1,0:T(8,128)S(1)}, u32[]{:S(2)}, u32[]{:S(2)}) %collective-permute-start) | collective-permute-done | bytes 524320 | tf_op jit(solution)/shard_map/ppermute | solution.py:14
  109.4 2.1 collective-permute-start.1
  111.5 10.5 %multiply_convert_fusion = bf16[8,512,512]{2,1,0:T(8,128)(2,1)} fusion(f32[8,512]{1,0:T(8,128)S(1)} %get-tuple-element.53, f32[8,512]{1,0:T(8,128)S(1)} %get-tuple-element.54, f32[8,512]{1,0:T(8,128)S(1)} %copy-done.9, f32[8,512]{1,0:T(8,128)S(1)} %copy-done.10, f32[8,512]{1,0:T(8,128)S(1)} %copy-done.11, f32[8,512]{1,0:T(8,128)S(1)} %copy-done.12, ...), kind=kOutput, calls=%fused_computation | convolution fusion | flops 566231040 | bytes 9338880 | tf_op jit(solution)/shard_map/while/body/eval_jaxpr/phe,she->hps/dot_general | solution.py:118
  122.0 3.7 %collective-permute-done.1 = f32[8,128,128]{2,1,0:T(8,128)S(1)} collective-permute-done((f32[8,128,128]{2,1,0:T(8,128)S(1)}, f32[8,128,128]{2,1,0:T(8,128)S(1)}, u32[]{:S(2)}, u32[]{:S(2)}) %collective-permute-start.1) | collective-permute-done | bytes 524320 | tf_op jit(solution)/shard_map/ppermute | solution.py:14
  125.8 1.6 collective-permute-start.2
  127.5 10.5 %multiply_convert_fusion.1 = bf16[8,512,512]{2,1,0:T(8,128)(2,1)} fusion(f32[8,512]{1,0:T(8,128)S(1)} %get-tuple-element.53, f32[8,512]{1,0:T(8,128)S(1)} %get-tuple-element.54, f32[8,512]{1,0:T(8,128)S(1)} %copy-done.9, f32[8,512]{1,0:T(8,128)S(1)} %copy-done.10, f32[8,512]{1,0:T(8,128)S(1)} %copy-done.11, f32[8,512]{1,0:T(8,128)S(1)} %copy-done.12, ...), kind=kOutput, calls=%fused_computation.1 | convolution fusion | flops 566231040 | bytes 9338880 | tf_op jit(solution)/shard_map/while/body/eval_jaxpr/phd,shd->hps/dot_general | solution.py:111
  137.9 30.2 %collective-permute-done.2 = f32[8,128,128]{2,1,0:T(8,128)S(1)} collective-permute-done((f32[8,128,128]{2,1,0:T(8,128)S(1)}, f32[8,128,128]{2,1,0:T(8,128)S(1)}, u32[]{:S(2)}, u32[]{:S(2)}) %collective-permute-start.2) | collective-permute-done | bytes 524320 | tf_op jit(solution)/shard_map/ppermute | solution.py:14
  168.2 0.7 copy-done.8
  168.9 2.3 fusion
  171.2 2.9 %copy.113 = f32[512,8,128]{2,0,1:T(8,128)} copy(f32[512,8,128]{0,2,1:T(8,128)} %fusion) | data formatting | bytes 4194304 | tf_op jit(solution)/shard_map/reduce_sum | solution.py:144
  174.1 4.1 %fusion.7 = bf16[512,8,128]{2,0,1:T(8,128)(2,1)S(1)} fusion(f32[512,8,128]{2,0,1:T(8,128)} %copy.113, bf16[8,512,512]{2,1,0:T(8,128)(2,1)} %multiply_convert_fusion, bf16[512,8,128]{2,1,0:T(8,128)(2,1)S(1)} %bitcast.130), kind=kOutput, calls=%fused_computation.16 | convolution fusion | flops 537919488 | bytes 8388608 | tf_op jit(solution)/shard_map/while/body/eval_jaxpr/hps,shd->phd/dot_general | solution.py:122
  178.2 1.6 copy.114
  179.9 2.3 convert_element_type.558
  182.1 4.5 %all-to-all-start.5 = ((bf16[4,128,1024]{2,1,0:T(8,128)(2,1)}), bf16[4,128,1024]{2,1,0:T(8,128)(2,1)}, u32[]{:S(2)}, u32[]{:S(2)}) async-start(bf16[4,128,1024]{2,1,0:T(8,128)(2,1)} %convert_element_type.558), calls=%async_computation.5 | async-start | bytes 2097152 | tf_op jit(solution)/shard_map/all_to_all | solution.py:172
  186.6 3.9 %fusion.1 = f32[512,8,128]{0,2,1:T(8,128)} fusion(f32[3,512,8]{1,0,2:T(4,128)S(1)} %copy.99, bf16[512,8,128,1]{2,1,0,3:T(8,128)(2,1)} %bitcast.137, bf16[1,8,128,128]{3,2,1,0:T(8,128)(2,1)} %copy-done.8, bf16[1,8,128,128]{3,2,1,0:T(8,128)(2,1)} %copy-done.7, bf16[1,8,128,128]{3,2,1,0:T(8,128)(2,1)S(1)} %copy-done.6), kind=kOutput, calls=%fused_computation.6 | convolution fusion | flops 406061056 | bytes 3981312 | tf_op jit(solution)/shard_map/phd,bhde->bphe/dot_general | solution.py:141
  190.5 2.9 %copy.104 = f32[512,8,128]{2,0,1:T(8,128)} copy(f32[512,8,128]{0,2,1:T(8,128)} %fusion.1) | data formatting | bytes 4194304 | tf_op jit(solution)/shard_map/reduce_sum | solution.py:139
  193.4 4.1 %fusion.8 = bf16[512,8,128]{2,0,1:T(8,128)(2,1)S(1)} fusion(f32[512,8,128]{2,0,1:T(8,128)} %copy.104, bf16[8,512,512]{2,1,0:T(8,128)(2,1)} %multiply_convert_fusion.1, bf16[512,8,128]{2,1,0:T(8,128)(2,1)S(1)} %bitcast.134), kind=kOutput, calls=%fused_computation.18 | convolution fusion | flops 537919488 | bytes 8388608 | tf_op jit(solution)/shard_map/while/body/eval_jaxpr/hps,she->phe/dot_general | solution.py:115
  197.6 1.6 copy.105
  199.2 2.3 convert_element_type.555
  201.5 4.3 %all-to-all-start.3 = ((bf16[4,128,1024]{2,1,0:T(8,128)(2,1)}), bf16[4,128,1024]{2,1,0:T(8,128)(2,1)}, u32[]{:S(2)}, u32[]{:S(2)}) async-start(bf16[4,128,1024]{2,1,0:T(8,128)(2,1)} %convert_element_type.555), calls=%async_computation.3 | async-start | bytes 2097152 | tf_op jit(solution)/shard_map/all_to_all | solution.py:171
  205.8 5.2 %fusion.16 = f32[8,512,128]{2,1,0:T(8,128)} fusion(bf16[8,512,512]{2,1,0:T(8,128)(2,1)} %multiply_convert_fusion, bf16[512,8,128]{2,1,0:T(8,128)(2,1)} %bitcast.138), kind=kOutput, calls=%fused_computation.33 | convolution fusion | flops 536870912 | bytes 7340032 | tf_op jit(solution)/shard_map/while/body/eval_jaxpr/hps,phd->shd/dot_general | solution.py:125
  211.0 1.1 convert_element_type.561
  212.1 2.0 fusion.6
  214.1 0.7 copy.124
  214.8 1.3 all_to_all.118
  216.1 4.2 %all-to-all-done.3 = bf16[4,128,1024]{2,1,0:T(8,128)(2,1)} async-done(((bf16[4,128,1024]{2,1,0:T(8,128)(2,1)}), bf16[4,128,1024]{2,1,0:T(8,128)(2,1)}, u32[]{:S(2)}, u32[]{:S(2)}) %all-to-all-start.3) | async-done | bytes 1048608 | tf_op jit(solution)/shard_map/all_to_all | solution.py:171
  220.3 3.5 %all-to-all-start.6 = ((bf16[4,128,1024]{2,1,0:T(8,128)(2,1)}), bf16[4,128,1024]{2,1,0:T(8,128)(2,1)S(1)}, u32[]{:S(2)}, u32[]{:S(2)}) async-start(bf16[4,128,1024]{2,1,0:T(8,128)(2,1)} %all_to_all.118), calls=%async_computation.7 | async-start | bytes 2097152 | tf_op jit(solution)/shard_map/all_to_all | solution.py:173
  223.8 3.6 %fusion.13 = f32[8,512,128]{2,1,0:T(8,128)S(1)} fusion(bf16[8,512,512]{2,1,0:T(8,128)(2,1)} %multiply_convert_fusion.1, bf16[512,8,128]{2,1,0:T(8,128)(2,1)S(1)} %bitcast.127), kind=kOutput, calls=%fused_computation.30 | convolution fusion | flops 536870912 | bytes 7340032 | tf_op jit(solution)/shard_map/while/body/eval_jaxpr/hps,phe->she/dot_general | solution.py:128
  227.8 0.7 copy.131
  228.5 1.3 all_to_all.122
  229.8 8.4 %all-to-all-done.6 = bf16[4,128,1024]{2,1,0:T(8,128)(2,1)S(1)} async-done(((bf16[4,128,1024]{2,1,0:T(8,128)(2,1)}), bf16[4,128,1024]{2,1,0:T(8,128)(2,1)S(1)}, u32[]{:S(2)}, u32[]{:S(2)}) %all-to-all-start.6) | async-done | bytes 1048608 | tf_op jit(solution)/shard_map/all_to_all | solution.py:173
  238.2 3.5 %all-to-all-start.7 = ((bf16[4,128,1024]{2,1,0:T(8,128)(2,1)}), bf16[4,128,1024]{2,1,0:T(8,128)(2,1)S(1)}, u32[]{:S(2)}, u32[]{:S(2)}) async-start(bf16[4,128,1024]{2,1,0:T(8,128)(2,1)} %all_to_all.122), calls=%async_computation.8 | async-start | bytes 2097152 | tf_op jit(solution)/shard_map/all_to_all | solution.py:174
  241.7 1.6 copy.115
  243.3 1.3 copy.134
  244.6 1.6 copy.106
  246.3 1.3 copy.133
  248.2 1.3 copy.135
  249.5 6.6 %all-to-all-done.7 = bf16[4,128,1024]{2,1,0:T(8,128)(2,1)S(1)} async-done(((bf16[4,128,1024]{2,1,0:T(8,128)(2,1)}), bf16[4,128,1024]{2,1,0:T(8,128)(2,1)S(1)}, u32[]{:S(2)}, u32[]{:S(2)}) %all-to-all-start.7) | async-done | bytes 1048608 | tf_op jit(solution)/shard_map/all_to_all | solution.py:174
  256.1 0.7 copy.132
  256.8 1.3 copy.136
  (53 shorter events, 3.3 us)
Async XLA Ops:
  7.2 6.8 %copy-start.2 = (bf16[128,4096]{1,0:T(8,128)(2,1)S(1)}, bf16[128,4096]{1,0:T(8,128)(2,1)}, u32[]{:S(2)}) copy-start(bf16[128,4096]{1,0:T(8,128)(2,1)} %param.8) | copy-start | bytes 3145732
  9.5 24.1 %copy-start.3 = (bf16[128,4096]{1,0:T(8,128)(2,1)S(1)}, bf16[128,4096]{1,0:T(8,128)(2,1)}, u32[]{:S(2)}) copy-start(bf16[128,4096]{1,0:T(8,128)(2,1)} %param.6) | copy-start | bytes 3145732
  9.5 18.8 %all-to-all-start = ((bf16[128,4,1024]{2,0,1:T(8,128)(2,1)}), bf16[128,4,1024]{2,0,1:T(8,128)(2,1)S(1)}, u32[]{:S(2)}, u32[]{:S(2)}) async-start(bf16[128,4,1024]{2,0,1:T(8,128)(2,1)} %bitcast.123), calls=%async_computation | async-start | bytes 2097152 | tf_op jit(solution)/shard_map/all_to_all | solution.py:33
  28.3 17.9 %all-to-all-start.4 = ((bf16[128,4,1024]{2,0,1:T(8,128)(2,1)}), bf16[128,4,1024]{2,0,1:T(8,128)(2,1)S(1)}, u32[]{:S(2)}, u32[]{:S(2)}) async-start(bf16[128,4,1024]{2,0,1:T(8,128)(2,1)} %bitcast.120), calls=%async_computation.4 | async-start | bytes 2097152 | tf_op jit(solution)/shard_map/all_to_all | solution.py:36
  46.3 22.1 %all-to-all-start.1 = ((bf16[128,4,1024]{2,0,1:T(8,128)(2,1)}), bf16[128,4,1024]{2,0,1:T(8,128)(2,1)}, u32[]{:S(2)}, u32[]{:S(2)}) async-start(bf16[128,4,1024]{2,0,1:T(8,128)(2,1)} %bitcast.122), calls=%async_computation.1 | async-start | bytes 2097152 | tf_op jit(solution)/shard_map/all_to_all | solution.py:34
  50.5 160.5 %reduce-scatter.2.cloned.1.call-start = ((), (), s32[]{:S(2)}) async-start(), calls=%async_computation.9 | async-start | bytes 4718592 | tf_op jit(solution)/shard_map/reduce_scatter | solution.py:83
  66.1 1.2 copy-start.4
  68.4 18.0 %all-to-all-start.2 = ((bf16[128,4,1024]{2,0,1:T(8,128)(2,1)}), bf16[128,4,1024]{2,0,1:T(8,128)(2,1)S(1)}, u32[]{:S(2)}, u32[]{:S(2)}) async-start(bf16[128,4,1024]{2,0,1:T(8,128)(2,1)} %bitcast.121), calls=%async_computation.2 | async-start | bytes 2097152 | tf_op jit(solution)/shard_map/all_to_all | solution.py:35
  86.4 1.0 copy-start.1
  88.9 22.5 %copy-start.9 = (f32[8,512]{1,0:T(8,128)S(1)}, f32[8,512]{1,0:T(8,128)}, u32[]{:S(2)}) copy-start(f32[8,512]{1,0:T(8,128)} %get-tuple-element.55) | copy-start | bytes 49156
  88.9 22.5 %copy-start.10 = (f32[8,512]{1,0:T(8,128)S(1)}, f32[8,512]{1,0:T(8,128)}, u32[]{:S(2)}) copy-start(f32[8,512]{1,0:T(8,128)} %get-tuple-element.56) | copy-start | bytes 49156
  88.9 22.5 %copy-start.11 = (f32[8,512]{1,0:T(8,128)S(1)}, f32[8,512]{1,0:T(8,128)}, u32[]{:S(2)}) copy-start(f32[8,512]{1,0:T(8,128)} %get-tuple-element.57) | copy-start | bytes 49156
  88.9 22.5 %copy-start.12 = (f32[8,512]{1,0:T(8,128)S(1)}, f32[8,512]{1,0:T(8,128)}, u32[]{:S(2)}) copy-start(f32[8,512]{1,0:T(8,128)} %get-tuple-element.58) | copy-start | bytes 49156
  89.0 22.5 %copy-start.13 = (f32[8,512]{1,0:T(8,128)S(1)}, f32[8,512]{1,0:T(8,128)}, u32[]{:S(2)}) copy-start(f32[8,512]{1,0:T(8,128)} %get-tuple-element.59) | copy-start | bytes 49156
  89.0 22.5 %copy-start.14 = (f32[8,512]{1,0:T(8,128)S(1)}, f32[8,512]{1,0:T(8,128)}, u32[]{:S(2)}) copy-start(f32[8,512]{1,0:T(8,128)} %get-tuple-element.60) | copy-start | bytes 49156
  89.0 22.5 %copy-start.15 = (f32[8,512]{1,0:T(8,128)S(1)}, f32[8,512]{1,0:T(8,128)}, u32[]{:S(2)}) copy-start(f32[8,512]{1,0:T(8,128)} %get-tuple-element.61) | copy-start | bytes 49156
  89.6 19.7 %collective-permute-start = (f32[8,128,128]{2,1,0:T(8,128)S(1)}, f32[8,128,128]{2,1,0:T(8,128)S(1)}, u32[]{:S(2)}, u32[]{:S(2)}) collective-permute-start(f32[8,128,128]{2,1,0:T(8,128)S(1)} %fusion.23), channel_id=1, source_target_pairs={{0,4},{4,0},{8,12},{12,8},{16,20},{20,16},{24,28},{28,24},{1,5},{5... | collective-permute-start | bytes 1572872 | tf_op jit(solution)/shard_map/ppermute | solution.py:14
  109.4 58.8 %copy-start.5 = (bf16[1,8,128,128]{3,2,1,0:T(8,128)(2,1)}, bf16[1,8,128,128]{3,2,1,0:T(8,128)(2,1)S(1)}, u32[]{:S(2)}) copy-start(bf16[1,8,128,128]{3,2,1,0:T(8,128)(2,1)S(1)} %get-tuple-element.45) | copy-start | bytes 786436
  109.4 16.4 %collective-permute-start.1 = (f32[8,128,128]{2,1,0:T(8,128)S(1)}, f32[8,128,128]{2,1,0:T(8,128)S(1)}, u32[]{:S(2)}, u32[]{:S(2)}) collective-permute-start(f32[8,128,128]{2,1,0:T(8,128)S(1)} %get-tuple-element.46), channel_id=1, source_target_pairs={{0,8},{8,0},{4,12},{12,4},{16,24},{24,16},{20,28},{28,20},{1,9},{9... | collective-permute-start | bytes 1572872 | tf_op jit(solution)/shard_map/ppermute | solution.py:14
  111.5 16.0 %copy-start = (bf16[64,8,8,128]{3,2,1,0:T(8,128)(2,1)S(1)}, bf16[64,8,8,128]{3,2,1,0:T(8,128)(2,1)}, u32[]{:S(2)}) copy-start(bf16[64,8,8,128]{3,2,1,0:T(8,128)(2,1)} %copy.158) | copy-start | bytes 3145732
  125.8 42.4 %copy-start.7 = (bf16[1,8,128,128]{3,2,1,0:T(8,128)(2,1)}, bf16[1,8,128,128]{3,2,1,0:T(8,128)(2,1)S(1)}, u32[]{:S(2)}) copy-start(bf16[1,8,128,128]{3,2,1,0:T(8,128)(2,1)S(1)} %get-tuple-element.47) | copy-start | bytes 786436
  125.8 42.3 %collective-permute-start.2 = (f32[8,128,128]{2,1,0:T(8,128)S(1)}, f32[8,128,128]{2,1,0:T(8,128)S(1)}, u32[]{:S(2)}, u32[]{:S(2)}) collective-permute-start(f32[8,128,128]{2,1,0:T(8,128)S(1)} %get-tuple-element.48), channel_id=1, source_target_pairs={{0,16},{16,0},{4,20},{20,4},{8,24},{24,8},{12,28},{28,12},{1,17},{... | collective-permute-start | bytes 1572872 | tf_op jit(solution)/shard_map/ppermute | solution.py:14
  168.2 0.7 copy-start.8
  178.2 8.4 %copy-start.6 = (bf16[1,8,128,128]{3,2,1,0:T(8,128)(2,1)S(1)}, bf16[1,8,128,128]{3,2,1,0:T(8,128)(2,1)}, u32[]{:S(2)}) copy-start(bf16[1,8,128,128]{3,2,1,0:T(8,128)(2,1)} %copy-done.5) | copy-start | bytes 786436
  182.1 19.4 %all-to-all-start.5 = ((bf16[4,128,1024]{2,1,0:T(8,128)(2,1)}), bf16[4,128,1024]{2,1,0:T(8,128)(2,1)}, u32[]{:S(2)}, u32[]{:S(2)}) async-start(bf16[4,128,1024]{2,1,0:T(8,128)(2,1)} %convert_element_type.558), calls=%async_computation.5 | async-start | bytes 2097152 | tf_op jit(solution)/shard_map/all_to_all | solution.py:172
  201.5 18.8 %all-to-all-start.3 = ((bf16[4,128,1024]{2,1,0:T(8,128)(2,1)}), bf16[4,128,1024]{2,1,0:T(8,128)(2,1)}, u32[]{:S(2)}, u32[]{:S(2)}) async-start(bf16[4,128,1024]{2,1,0:T(8,128)(2,1)} %convert_element_type.555), calls=%async_computation.3 | async-start | bytes 2097152 | tf_op jit(solution)/shard_map/all_to_all | solution.py:171
  220.3 17.9 %all-to-all-start.6 = ((bf16[4,128,1024]{2,1,0:T(8,128)(2,1)}), bf16[4,128,1024]{2,1,0:T(8,128)(2,1)S(1)}, u32[]{:S(2)}, u32[]{:S(2)}) async-start(bf16[4,128,1024]{2,1,0:T(8,128)(2,1)} %all_to_all.118), calls=%async_computation.7 | async-start | bytes 2097152 | tf_op jit(solution)/shard_map/all_to_all | solution.py:173
  238.2 17.9 %all-to-all-start.7 = ((bf16[4,128,1024]{2,1,0:T(8,128)(2,1)}), bf16[4,128,1024]{2,1,0:T(8,128)(2,1)S(1)}, u32[]{:S(2)}, u32[]{:S(2)}) async-start(bf16[4,128,1024]{2,1,0:T(8,128)(2,1)} %all_to_all.122), calls=%async_computation.8 | async-start | bytes 2097152 | tf_op jit(solution)/shard_map/all_to_all | solution.py:174
Sparse Core Ops, SparseCore 0:
  66.3 102.7 reduce-scatter.1
where the time goes:
time: 266 us; the launch traced here: 265 us
  waiting for transfers between devices  104 us (39%)
  matrix products  55.8 us (21%)
  local copies, waits for them, and re-layouts  46.9 us (18%)
  starting transfers between devices  37.6 us (14%)
  between operations  14.6 us (5%)
  other arithmetic  6.23 us (2%)
    ppermute x3, waiting for transfers between devices, swapped(): return lax.ppermute(block, axis, route)  48.2 us
    all_to_all x1, waiting for transfers between devices, on_device(): lax.all_to_all(query_input, 'head', split_axis=1, concat_axis=0, tiled=True)  13.4 us
    all_to_all x1, waiting for transfers between devices, on_device(): lax.all_to_all(value_input, 'head', split_axis=1, concat_axis=0, tiled=True)  12.7 us
    unnamed x40, local copies, waits for them, and re-layouts  12.7 us
    dot_general x1, matrix products, row_step(): jnp.einsum('phe,she->hps', cot_heads, value_heads, preferred_element_type...  10.5 us
    dot_general x1, matrix products, row_step(): jnp.einsum('phd,shd->hps', query_heads, key_heads, preferred_element_type...  10.5 us
    all_to_all x1, waiting for transfers between devices, on_device(): lax.all_to_all(cotangent, 'head', split_axis=1, concat_axis=0, tiled=True)  10.3 us
    all_to_all x1, waiting for transfers between devices, on_device(): lax.all_to_all(grad_key, 'head', split_axis=0, concat_axis=1, tiled=True)  8.37 us
  transfers between devices with their start and end apart: 12, of which 9 were waited for; matrix products, arithmetic and copies ran while one was open for 37% of the time, Pallas kernels for 0%

commit v1 on v0

--- a/solution.py
+++ b/solution.py
@@ -2,6 +2,22 @@
 import jax.numpy as jnp
 from jax import lax
 from jax.sharding import PartitionSpec as P
+
+
+def exchange_in_pairs(array, axis, split, join):
+    ways, here = (lax.axis_size(axis), lax.axis_index(axis))
+    width = array.shape[split] // ways
+    shape = list(array.shape)
+    shape[split] = width
+    height = shape[join]
+    shape[join] = height * ways
+    full = jnp.zeros(shape, array.dtype)
+    for mask in range(ways):
+        part = lax.dynamic_slice_in_dim(array, (here ^ mask) * width, width, axis=split)
+        if mask:
+            part = lax.ppermute(part, axis, [(d, d ^ mask) for d in range(ways)])
+        full = lax.dynamic_update_slice_in_dim(full, part, (here ^ mask) * height, axis=join)
+    return full
 
 
 def swapped(block, axis, stride):
@@ -33,7 +49,7 @@
         lax.all_to_all(query_input, "head", split_axis=1, concat_axis=0, tiled=True),
         lax.all_to_all(key_input, "head", split_axis=1, concat_axis=0, tiled=True),
         lax.all_to_all(value_input, "head", split_axis=1, concat_axis=0, tiled=True),
-        lax.all_to_all(cotangent, "head", split_axis=1, concat_axis=0, tiled=True),
+        exchange_in_pairs(cotangent, "head", 1, 0),
     )
     head_count = level_codes.shape[0]
     total_levels = level_codes.shape[1]

time: 266 us -> 253 us (0.951)
  waiting for transfers between devices: 104 us -> 89.5 us
  matrix products: 55.8 us -> 48.7 us
  local copies, waits for them, and re-layouts: 46.9 us -> 52.7 us
  other arithmetic: 6.23 us -> 9.92 us
    all_to_all x1 -> x0, waiting for transfers between devices: 10.3 us -> none  [on_device(): lax.all_to_all(cotangent, 'head', split_axis=1, concat_axis=0, tiled=True)]
    ppermute x3, waiting for transfers between devices: 48.2 us -> 43.9 us  [swapped(): return lax.ppermute(block, axis, route)]
    all_to_all x1, waiting for transfers between devices: 13.4 us -> 9.36 us  [on_device(): lax.all_to_all(query_input, 'head', split_axis=1, concat_axis=0, tiled=True)]
    all_to_all x1, waiting for transfers between devices: 4.18 us -> 7.82 us  [on_device(): lax.all_to_all(attended, 'head', split_axis=0, concat_axis=1, tiled=True)]
    all_to_all x1 -> x0, starting transfers between devices: 3.52 us -> none  [on_device(): lax.all_to_all(cotangent, 'head', split_axis=1, concat_axis=0, tiled=True)]
    ppermute x0 -> x3, starting transfers between devices: none -> 3.08 us  [exchange_in_pairs(): part = lax.ppermute(part, axis, [(d, d ^ mask) for d in range(ways)])]
    unnamed x40 -> x49, local copies, waits for them, and re-layouts: 12.7 us -> 15 us
  transfers between devices with their start and end apart: 12 -> 14, of which waited for: 9 -> 9; matrix products, arithmetic and copies ran while one was open for 37% -> 39% of each run, Pallas kernels for 0% -> 0%
where the time goes in v1:
time: 253 us; the launch traced here: 251 us
  waiting for transfers between devices  89.5 us (35%)
  local copies, waits for them, and re-layouts  52.7 us (21%)
  matrix products  48.7 us (19%)
  starting transfers between devices  35.9 us (14%)
  between operations  14.7 us (6%)
  other arithmetic  9.92 us (4%)
    ppermute x3, waiting for transfers between devices, swapped(): return lax.ppermute(block, axis, route)  43.9 us
    unnamed x49, local copies, waits for them, and re-layouts  15 us
    all_to_all x1, waiting for transfers between devices, on_device(): lax.all_to_all(value_input, 'head', split_axis=1, concat_axis=0, tiled=True)  12.7 us
    dot_general x1, matrix products, row_step(): jnp.einsum('phd,shd->hps', query_heads, key_heads, preferred_element_type...  10.6 us
    dot_general x1, matrix products, row_step(): jnp.einsum('phe,she->hps', cot_heads, value_heads, preferred_element_type...  10 us
    all_to_all x1, waiting for transfers between devices, on_device(): lax.all_to_all(query_input, 'head', split_axis=1, concat_axis=0, tiled=True)  9.36 us
    all_to_all x1, waiting for transfers between devices, on_device(): lax.all_to_all(grad_value, 'head', split_axis=0, concat_axis=1, tiled=True)  8.35 us
    all_to_all x1, waiting for transfers between devices, on_device(): lax.all_to_all(attended, 'head', split_axis=0, concat_axis=1, tiled=True)  7.82 us
  transfers between devices with their start and end apart: 14, of which 9 were waited for; matrix products, arithmetic and copies ran while one was open for 39% of the time, Pallas kernels for 0%

profile of v1, /device:TPU:0, one launch (start us, length us, event | category | flops | bytes accessed | tf_op | source)
XLA Modules:
  0.0 251.4 jit_solution(4446103981617654276)
XLA Ops:
  7.3 2.1 constant_dynamic-slice_fusion
  9.9 2.5 collective-permute-start.4
  12.5 2.3 copy.190
  14.8 3.5 %all-to-all-start = ((bf16[128,4,1024]{2,0,1:T(8,128)(2,1)}), bf16[128,4,1024]{2,0,1:T(8,128)(2,1)S(1)}, u32[]{:S(2)}, u32[]{:S(2)}) async-start(bf16[128,4,1024]{2,0,1:T(8,128)(2,1)} %bitcast.119), calls=%async_computation | async-start | bytes 2097152 | tf_op jit(solution)/shard_map/all_to_all | solution.py:49
  20.3 2.3 copy.189
  22.6 1.1 copy.108
  23.8 1.1 copy.109
  25.4 1.6 convert_element_type.562
  27.1 9.4 %all-to-all-done = bf16[128,4,1024]{2,0,1:T(8,128)(2,1)S(1)} async-done(((bf16[128,4,1024]{2,0,1:T(8,128)(2,1)}), bf16[128,4,1024]{2,0,1:T(8,128)(2,1)S(1)}, u32[]{:S(2)}, u32[]{:S(2)}) %all-to-all-start) | async-done | bytes 1048608 | tf_op jit(solution)/shard_map/all_to_all | solution.py:49
  36.4 4.3 %all-to-all-start.1 = ((bf16[128,4,1024]{2,0,1:T(8,128)(2,1)}), bf16[128,4,1024]{2,0,1:T(8,128)(2,1)}, u32[]{:S(2)}, u32[]{:S(2)}) async-start(bf16[128,4,1024]{2,0,1:T(8,128)(2,1)} %bitcast.118), calls=%async_computation.1 | async-start | bytes 2097152 | tf_op jit(solution)/shard_map/all_to_all | solution.py:50
  41.0 1.0 copy-done.2
  42.0 3.7 %fusion.8 = f32[3,8,128,128]{2,3,0,1:T(8,128)} fusion(f32[512,8,128]{0,2,1:T(8,128)} %convert_element_type.562, f32[3,512,8]{1,0,2:T(4,128)S(1)} %copy.99, bf16[512,8,128,1]{2,1,0,3:T(8,128)(2,1)S(1)} %bitcast.133), kind=kOutput, calls=%fused_computation.18 | convolution fusion | flops 405798912 | bytes 4767744 | tf_op jit(solution)/shard_map/phd,bphe->bhde/dot_general | solution.py:81
  45.7 2.0 copy.122
  47.7 4.4 %fusion.51 = f32[8,8,128,128]{3,0,2,1:T(8,128)S(1)} fusion(f32[3,8,128,128]{3,0,2,1:T(4,128)S(1)} %copy.122, f32[8,1]{0,1:T(1,128)S(1)} %and_select_fusion, f32[8,1]{0,1:T(1,128)S(1)} %copy-done.20, f32[8,1]{0,1:T(1,128)S(1)} %and_select_fusion.6), kind=kOutput, calls=%fused_computation.127 | convolution fusion | flops 37748784 | bytes 5767264 | tf_op jit(solution)/shard_map/tb,bhde->thde/dot_general | solution.py:98
  52.2 2.7 %copy.123 = f32[8,8,128,128]{3,2,1,0:T(8,128)} copy(f32[8,8,128,128]{3,0,2,1:T(8,128)S(1)} %fusion.51) | data formatting | bytes 8388608 | tf_op jit(solution)/shard_map/tb,bhde->thde/dot_general | solution.py:98
  54.9 1.2 copy-done.6
  56.1 1.1 copy.188
  57.2 3.7 %all-to-all-start.2 = ((bf16[128,4,1024]{2,0,1:T(8,128)(2,1)}), bf16[128,4,1024]{2,0,1:T(8,128)(2,1)S(1)}, u32[]{:S(2)}, u32[]{:S(2)}) async-start(bf16[128,4,1024]{2,0,1:T(8,128)(2,1)} %bitcast.117), calls=%async_computation.2 | async-start | bytes 2097152 | tf_op jit(solution)/shard_map/all_to_all | solution.py:51
  61.0 1.5 copy.155
  62.5 12.7 %all-to-all-done.2 = bf16[128,4,1024]{2,0,1:T(8,128)(2,1)S(1)} async-done(((bf16[128,4,1024]{2,0,1:T(8,128)(2,1)}), bf16[128,4,1024]{2,0,1:T(8,128)(2,1)S(1)}, u32[]{:S(2)}, u32[]{:S(2)}) %all-to-all-start.2) | async-done | bytes 1048608 | tf_op jit(solution)/shard_map/all_to_all | solution.py:51
  75.2 1.0 copy-done.5
  76.2 1.5 copy.156
  78.4 1.8 collective-permute-start
  80.2 3.0 %broadcast_compare_fusion.9 = (pred[512,512]{1,0:T(8,128)(4,1)S(1)}, pred[512,512]{1,0:T(8,128)(4,1)S(1)}, pred[512,512]{1,0:T(8,128)(4,1)S(1)}, pred[512,512]{1...) fusion(s32[512]{0:T(512)S(1)} %get-tuple-element.76, ...), kind=kLoop, calls=%fused_computation.57 | loop fusion | flops 9437184 | bytes 2637824 | tf_op jit(solution)/shard_map/while/body/eval_jaxpr/eq | solution.py:122
  83.2 14.3 %collective-permute-done = f32[8,128,128]{2,1,0:T(8,128)S(1)} collective-permute-done((f32[8,128,128]{2,1,0:T(8,128)S(1)}, f32[8,128,128]{2,1,0:T(8,128)S(1)}, u32[]{:S(2)}, u32[]{:S(2)}) %collective-permute-start) | collective-permute-done | bytes 524320 | tf_op jit(solution)/shard_map/ppermute | solution.py:30
  97.7 2.1 collective-permute-start.1
  99.8 10.6 %multiply_convert_fusion.1 = bf16[8,512,512]{2,1,0:T(8,128)(2,1)} fusion(f32[8,512]{1,0:T(8,128)S(1)} %get-tuple-element.57, f32[8,512]{1,0:T(8,128)S(1)} %copy-done.12, f32[8,512]{1,0:T(8,128)S(1)} %copy-done.13, f32[8,512]{1,0:T(8,128)S(1)} %copy-done.14, f32[8,512]{1,0:T(8,128)S(1)} %copy-done.15, f32[8,512]{1,0:T(8,128)S(1)} %copy-done.16, ...), kind=kOutput, calls=%fused_computation.1 | convolution fusion | flops 566231040 | bytes 9338880 | tf_op jit(solution)/shard_map/while/body/eval_jaxpr/phd,shd->hps/dot_general | solution.py:127
  110.4 3.5 %collective-permute-done.1 = f32[8,128,128]{2,1,0:T(8,128)S(1)} collective-permute-done((f32[8,128,128]{2,1,0:T(8,128)S(1)}, f32[8,128,128]{2,1,0:T(8,128)S(1)}, u32[]{:S(2)}, u32[]{:S(2)}) %collective-permute-start.1) | collective-permute-done | bytes 524320 | tf_op jit(solution)/shard_map/ppermute | solution.py:30
  114.0 1.6 collective-permute-start.2
  115.7 10.0 %multiply_convert_fusion = bf16[8,512,512]{2,1,0:T(8,128)(2,1)S(1)} fusion(f32[8,512]{1,0:T(8,128)S(1)} %get-tuple-element.57, f32[8,512]{1,0:T(8,128)S(1)} %copy-done.12, f32[8,512]{1,0:T(8,128)S(1)} %copy-done.13, f32[8,512]{1,0:T(8,128)S(1)} %copy-done.14, f32[8,512]{1,0:T(8,128)S(1)} %copy-done.15, f32[8,512]{1,0:T(8,128)S(1)} %copy-done.16, ...), kind=kOutput, calls=%fused_computation | convolution fusion | flops 566231040 | bytes 9338880 | tf_op jit(solution)/shard_map/while/body/eval_jaxpr/phe,she->hps/dot_general | solution.py:134
  125.7 2.0 copy-done
  127.7 2.6 %fusion.25 = f32[8,512,128]{2,1,0:T(8,128)} fusion(bf16[8,512,512]{2,1,0:T(8,128)(2,1)S(1)} %multiply_convert_fusion, bf16[512,8,128]{2,1,0:T(8,128)(2,1)S(1)} %bitcast.123), kind=kOutput, calls=%fused_computation.42 | convolution fusion | flops 536870912 | bytes 7340032 | tf_op jit(solution)/shard_map/while/body/eval_jaxpr/hps,shd->phd/dot_general | solution.py:138
  130.3 26.0 %collective-permute-done.2 = f32[8,128,128]{2,1,0:T(8,128)S(1)} collective-permute-done((f32[8,128,128]{2,1,0:T(8,128)S(1)}, f32[8,128,128]{2,1,0:T(8,128)S(1)}, u32[]{:S(2)}, u32[]{:S(2)}) %collective-permute-start.2) | collective-permute-done | bytes 524320 | tf_op jit(solution)/shard_map/ppermute | solution.py:30
  156.4 0.7 copy-done.10
  157.1 2.3 fusion
  159.4 2.9 %copy.116 = f32[512,8,128]{2,0,1:T(8,128)} copy(f32[512,8,128]{0,2,1:T(8,128)} %fusion) | data formatting | bytes 4194304 | tf_op jit(solution)/shard_map/reduce_sum | solution.py:160
  162.3 2.4 fusion.6
  164.7 1.6 copy.117
  166.4 2.3 convert_element_type.561
  168.7 4.5 %all-to-all-start.4 = ((bf16[4,128,1024]{2,1,0:T(8,128)(2,1)}), bf16[4,128,1024]{2,1,0:T(8,128)(2,1)}, u32[]{:S(2)}, u32[]{:S(2)}) async-start(bf16[4,128,1024]{2,1,0:T(8,128)(2,1)} %convert_element_type.561), calls=%async_computation.4 | async-start | bytes 2097152 | tf_op jit(solution)/shard_map/all_to_all | solution.py:188
  173.1 3.9 %fusion.1 = f32[512,8,128]{0,2,1:T(8,128)} fusion(f32[3,512,8]{1,0,2:T(4,128)S(1)} %copy.99, bf16[512,8,128,1]{2,1,0,3:T(8,128)(2,1)} %bitcast.134, bf16[1,8,128,128]{3,2,1,0:T(8,128)(2,1)} %copy-done.10, bf16[1,8,128,128]{3,2,1,0:T(8,128)(2,1)} %copy-done.9, bf16[1,8,128,128]{3,2,1,0:T(8,128)(2,1)S(1)} %copy-done.8), kind=kOutput, calls=%fused_computation.6 | convolution fusion | flops 406061056 | bytes 3981312 | tf_op jit(solution)/shard_map/phd,bhde->bphe/dot_general | solution.py:157
  177.0 2.9 %copy.104 = f32[512,8,128]{2,0,1:T(8,128)} copy(f32[512,8,128]{0,2,1:T(8,128)} %fusion.1) | data formatting | bytes 4194304 | tf_op jit(solution)/shard_map/reduce_sum | solution.py:155
  179.9 4.1 %fusion.7 = bf16[512,8,128]{2,0,1:T(8,128)(2,1)S(1)} fusion(f32[512,8,128]{2,0,1:T(8,128)} %copy.104, bf16[8,512,512]{2,1,0:T(8,128)(2,1)} %multiply_convert_fusion.1, bf16[512,8,128]{2,1,0:T(8,128)(2,1)S(1)} %bitcast.127), kind=kOutput, calls=%fused_computation.16 | convolution fusion | flops 537919488 | bytes 8388608 | tf_op jit(solution)/shard_map/while/body/eval_jaxpr/hps,she->phe/dot_general | solution.py:131
  184.0 1.6 copy.105
  185.7 2.3 convert_element_type.558
  188.0 4.3 %all-to-all-start.3 = ((bf16[4,128,1024]{2,1,0:T(8,128)(2,1)}), bf16[4,128,1024]{2,1,0:T(8,128)(2,1)}, u32[]{:S(2)}, u32[]{:S(2)}) async-start(bf16[4,128,1024]{2,1,0:T(8,128)(2,1)} %convert_element_type.558), calls=%async_computation.3 | async-start | bytes 2097152 | tf_op jit(solution)/shard_map/all_to_all | solution.py:187
  192.3 1.2 convert_element_type.564
  194.6 1.8 fusion.9
  196.4 1.4 all_to_all.107
  197.8 1.1 copy.130
  198.9 7.8 %all-to-all-done.3 = bf16[4,128,1024]{2,1,0:T(8,128)(2,1)} async-done(((bf16[4,128,1024]{2,1,0:T(8,128)(2,1)}), bf16[4,128,1024]{2,1,0:T(8,128)(2,1)}, u32[]{:S(2)}, u32[]{:S(2)}) %all-to-all-start.3) | async-done | bytes 1048608 | tf_op jit(solution)/shard_map/all_to_all | solution.py:187
  206.8 3.5 %all-to-all-start.6 = ((bf16[4,128,1024]{1,2,0:T(8,128)(2,1)}), bf16[4,128,1024]{1,2,0:T(8,128)(2,1)S(1)}, u32[]{:S(2)}, u32[]{:S(2)}) async-start(bf16[4,128,1024]{1,2,0:T(8,128)(2,1)} %copy.130), calls=%async_computation.7 | async-start | bytes 2097152 | tf_op jit(solution)/shard_map/all_to_all | solution.py:190
  210.3 3.6 %fusion.12 = f32[8,512,128]{2,1,0:T(8,128)S(1)} fusion(bf16[8,512,512]{2,1,0:T(8,128)(2,1)} %copy-done, bf16[512,8,128]{2,1,0:T(8,128)(2,1)S(1)} %bitcast.136), kind=kOutput, calls=%fused_computation.28 | convolution fusion | flops 536870912 | bytes 7340032 | tf_op jit(solution)/shard_map/while/body/eval_jaxpr/hps,phd->shd/dot_general | solution.py:141
  214.4 0.7 copy.126
  215.1 1.3 all_to_all.103
  216.3 8.3 %all-to-all-done.6 = bf16[4,128,1024]{1,2,0:T(8,128)(2,1)S(1)} async-done(((bf16[4,128,1024]{1,2,0:T(8,128)(2,1)}), bf16[4,128,1024]{1,2,0:T(8,128)(2,1)S(1)}, u32[]{:S(2)}, u32[]{:S(2)}) %all-to-all-start.6) | async-done | bytes 1048608 | tf_op jit(solution)/shard_map/all_to_all | solution.py:190
  224.7 3.5 %all-to-all-start.5 = ((bf16[4,128,1024]{2,1,0:T(8,128)(2,1)}), bf16[4,128,1024]{2,1,0:T(8,128)(2,1)S(1)}, u32[]{:S(2)}, u32[]{:S(2)}) async-start(bf16[4,128,1024]{2,1,0:T(8,128)(2,1)} %all_to_all.103), calls=%async_computation.6 | async-start | bytes 2097152 | tf_op jit(solution)/shard_map/all_to_all | solution.py:189
  228.2 1.6 copy.118
  229.8 1.3 copy.132
  231.1 1.6 copy.106
  232.8 1.3 copy.131
  234.1 1.3 copy.134
  235.4 7.2 %all-to-all-done.5 = bf16[4,128,1024]{2,1,0:T(8,128)(2,1)S(1)} async-done(((bf16[4,128,1024]{2,1,0:T(8,128)(2,1)}), bf16[4,128,1024]{2,1,0:T(8,128)(2,1)S(1)}, u32[]{:S(2)}, u32[]{:S(2)}) %all-to-all-start.5) | async-done | bytes 1048608 | tf_op jit(solution)/shard_map/all_to_all | solution.py:189
  243.3 1.3 copy.133
  (73 shorter events, 6.7 us)
Async XLA Ops:
  7.2 11.2 %copy-start.11 = (s32[8,13,512]{2,0,1:T(8,128)S(1)}, s32[8,13,512]{2,0,1:T(8,128)}, u32[]{:S(2)}) copy-start(s32[8,13,512]{2,0,1:T(8,128)} %param.9) | copy-start | bytes 638980
  9.4 13.2 %collective-permute-start.3 = (bf16[128,1024]{1,0:T(8,128)(2,1)}, bf16[128,1024]{1,0:T(8,128)(2,1)}, u32[]{:S(2)}, u32[]{:S(2)}) collective-permute-start(bf16[128,1024]{1,0:T(8,128)(2,1)} %get-tuple-element.46), channel_id=1, source_target_pairs={{0,1},{1,0},{2,3},{3,2},{4,5},{5,4},{6,7},{7,6},{8,9},{9,8},{10,11... | collective-permute-start | bytes 786440 | tf_op jit(solution)/shard_map/ppermute | solution.py:18
  9.9 13.9 %collective-permute-start.4 = (bf16[128,1024]{1,0:T(8,128)(2,1)}, bf16[128,1024]{1,0:T(8,128)(2,1)}, u32[]{:S(2)}, u32[]{:S(2)}) collective-permute-start(bf16[128,1024]{1,0:T(8,128)(2,1)} %get-tuple-element.48), channel_id=1, source_target_pairs={{0,2},{1,3},{2,0},{3,1},{4,6},{5,7},{6,4},{7,5},{8,10},{9,11},{10,... | collective-permute-start | bytes 786440 | tf_op jit(solution)/shard_map/ppermute | solution.py:18
  12.4 12.6 %collective-permute-start.5 = (bf16[128,1024]{1,0:T(8,128)(2,1)}, bf16[128,1024]{1,0:T(8,128)(2,1)S(1)}, u32[]{:S(2)}, u32[]{:S(2)}) collective-permute-start(bf16[128,1024]{1,0:T(8,128)(2,1)} %get-tuple-element.45), channel_id=1, source_target_pairs={{0,3},{1,2},{2,1},{3,0},{4,7},{5,6},{6,5},{7,4},{8,11},{9,10},{10,... | collective-permute-start | bytes 786440 | tf_op jit(solution)/shard_map/ppermute | solution.py:18
  14.8 21.6 %all-to-all-start = ((bf16[128,4,1024]{2,0,1:T(8,128)(2,1)}), bf16[128,4,1024]{2,0,1:T(8,128)(2,1)S(1)}, u32[]{:S(2)}, u32[]{:S(2)}) async-start(bf16[128,4,1024]{2,0,1:T(8,128)(2,1)} %bitcast.119), calls=%async_computation | async-start | bytes 2097152 | tf_op jit(solution)/shard_map/all_to_all | solution.py:49
  36.4 20.7 %all-to-all-start.1 = ((bf16[128,4,1024]{2,0,1:T(8,128)(2,1)}), bf16[128,4,1024]{2,0,1:T(8,128)(2,1)}, u32[]{:S(2)}, u32[]{:S(2)}) async-start(bf16[128,4,1024]{2,0,1:T(8,128)(2,1)} %bitcast.118), calls=%async_computation.1 | async-start | bytes 2097152 | tf_op jit(solution)/shard_map/all_to_all | solution.py:50
  40.7 151.6 %reduce-scatter.2.cloned.1.call-start = ((), (), s32[]{:S(2)}) async-start(), calls=%async_computation.8 | async-start | bytes 4718592 | tf_op jit(solution)/shard_map/reduce_scatter | solution.py:99
  41.0 1.0 copy-start.2
  42.0 5.7 %copy-start.20 = (f32[8,1]{0,1:T(1,128)S(1)}, f32[8,1]{0,1:T(1,128)}, u32[]{:S(2)}) copy-start(f32[8,1]{0,1:T(1,128)} %and_select_fusion.3) | copy-start | bytes 100
  54.9 1.2 copy-start.6
  57.2 18.0 %all-to-all-start.2 = ((bf16[128,4,1024]{2,0,1:T(8,128)(2,1)}), bf16[128,4,1024]{2,0,1:T(8,128)(2,1)S(1)}, u32[]{:S(2)}, u32[]{:S(2)}) async-start(bf16[128,4,1024]{2,0,1:T(8,128)(2,1)} %bitcast.117), calls=%async_computation.2 | async-start | bytes 2097152 | tf_op jit(solution)/shard_map/all_to_all | solution.py:51
  75.2 1.0 copy-start.5
  77.7 22.1 %copy-start.3 = (bf16[64,8,8,128]{3,2,1,0:T(8,128)(2,1)S(1)}, bf16[64,8,8,128]{3,2,1,0:T(8,128)(2,1)}, u32[]{:S(2)}) copy-start(bf16[64,8,8,128]{3,2,1,0:T(8,128)(2,1)} %copy-done.2) | copy-start | bytes 3145732
  77.7 22.1 %copy-start.12 = (f32[8,512]{1,0:T(8,128)S(1)}, f32[8,512]{1,0:T(8,128)}, u32[]{:S(2)}) copy-start(f32[8,512]{1,0:T(8,128)} %get-tuple-element.58) | copy-start | bytes 49156
  77.7 22.1 %copy-start.13 = (f32[8,512]{1,0:T(8,128)S(1)}, f32[8,512]{1,0:T(8,128)}, u32[]{:S(2)}) copy-start(f32[8,512]{1,0:T(8,128)} %get-tuple-element.59) | copy-start | bytes 49156
  77.7 22.1 %copy-start.14 = (f32[8,512]{1,0:T(8,128)S(1)}, f32[8,512]{1,0:T(8,128)}, u32[]{:S(2)}) copy-start(f32[8,512]{1,0:T(8,128)} %get-tuple-element.60) | copy-start | bytes 49156
  77.7 22.1 %copy-start.15 = (f32[8,512]{1,0:T(8,128)S(1)}, f32[8,512]{1,0:T(8,128)}, u32[]{:S(2)}) copy-start(f32[8,512]{1,0:T(8,128)} %get-tuple-element.61) | copy-start | bytes 49156
  77.7 22.1 %copy-start.16 = (f32[8,512]{1,0:T(8,128)S(1)}, f32[8,512]{1,0:T(8,128)}, u32[]{:S(2)}) copy-start(f32[8,512]{1,0:T(8,128)} %get-tuple-element.62) | copy-start | bytes 49156
  77.7 22.1 %copy-start.17 = (f32[8,512]{1,0:T(8,128)S(1)}, f32[8,512]{1,0:T(8,128)}, u32[]{:S(2)}) copy-start(f32[8,512]{1,0:T(8,128)} %get-tuple-element.63) | copy-start | bytes 49156
  77.7 22.1 %copy-start.18 = (f32[8,512]{1,0:T(8,128)S(1)}, f32[8,512]{1,0:T(8,128)}, u32[]{:S(2)}) copy-start(f32[8,512]{1,0:T(8,128)} %get-tuple-element.64) | copy-start | bytes 49156
  77.8 22.1 %copy-start.19 = (f32[8,512]{1,0:T(8,128)S(1)}, f32[8,512]{1,0:T(8,128)}, u32[]{:S(2)}) copy-start(f32[8,512]{1,0:T(8,128)} %get-tuple-element.65) | copy-start | bytes 49156
  78.4 19.2 %collective-permute-start = (f32[8,128,128]{2,1,0:T(8,128)S(1)}, f32[8,128,128]{2,1,0:T(8,128)S(1)}, u32[]{:S(2)}, u32[]{:S(2)}) collective-permute-start(f32[8,128,128]{2,1,0:T(8,128)S(1)} %fusion.19), channel_id=1, source_target_pairs={{0,4},{4,0},{8,12},{12,8},{16,20},{20,16},{24,28},{28,24},{1,5},{5... | collective-permute-start | bytes 1572872 | tf_op jit(solution)/shard_map/ppermute | solution.py:30
  97.6 58.7 %copy-start.7 = (bf16[1,8,128,128]{3,2,1,0:T(8,128)(2,1)}, bf16[1,8,128,128]{3,2,1,0:T(8,128)(2,1)S(1)}, u32[]{:S(2)}) copy-start(bf16[1,8,128,128]{3,2,1,0:T(8,128)(2,1)S(1)} %get-tuple-element.49) | copy-start | bytes 786436
  97.7 16.3 %collective-permute-start.1 = (f32[8,128,128]{2,1,0:T(8,128)S(1)}, f32[8,128,128]{2,1,0:T(8,128)S(1)}, u32[]{:S(2)}, u32[]{:S(2)}) collective-permute-start(f32[8,128,128]{2,1,0:T(8,128)S(1)} %get-tuple-element.50), channel_id=1, source_target_pairs={{0,8},{8,0},{4,12},{12,4},{16,24},{24,16},{20,28},{28,20},{1,9},{9... | collective-permute-start | bytes 1572872 | tf_op jit(solution)/shard_map/ppermute | solution.py:30
  114.0 42.3 %copy-start.9 = (bf16[1,8,128,128]{3,2,1,0:T(8,128)(2,1)}, bf16[1,8,128,128]{3,2,1,0:T(8,128)(2,1)S(1)}, u32[]{:S(2)}) copy-start(bf16[1,8,128,128]{3,2,1,0:T(8,128)(2,1)S(1)} %get-tuple-element.51) | copy-start | bytes 786436
  114.0 42.3 %collective-permute-start.2 = (f32[8,128,128]{2,1,0:T(8,128)S(1)}, f32[8,128,128]{2,1,0:T(8,128)S(1)}, u32[]{:S(2)}, u32[]{:S(2)}) collective-permute-start(f32[8,128,128]{2,1,0:T(8,128)S(1)} %get-tuple-element.52), channel_id=1, source_target_pairs={{0,16},{16,0},{4,20},{20,4},{8,24},{24,8},{12,28},{28,12},{1,17},{... | collective-permute-start | bytes 1572872 | tf_op jit(solution)/shard_map/ppermute | solution.py:30
  125.7 2.0 copy-start
  156.4 0.7 copy-start.10
  164.7 8.4 %copy-start.8 = (bf16[1,8,128,128]{3,2,1,0:T(8,128)(2,1)S(1)}, bf16[1,8,128,128]{3,2,1,0:T(8,128)(2,1)}, u32[]{:S(2)}) copy-start(bf16[1,8,128,128]{3,2,1,0:T(8,128)(2,1)} %copy-done.7) | copy-start | bytes 786436
  168.7 19.3 %all-to-all-start.4 = ((bf16[4,128,1024]{2,1,0:T(8,128)(2,1)}), bf16[4,128,1024]{2,1,0:T(8,128)(2,1)}, u32[]{:S(2)}, u32[]{:S(2)}) async-start(bf16[4,128,1024]{2,1,0:T(8,128)(2,1)} %convert_element_type.561), calls=%async_computation.4 | async-start | bytes 2097152 | tf_op jit(solution)/shard_map/all_to_all | solution.py:188
  188.0 18.8 %all-to-all-start.3 = ((bf16[4,128,1024]{2,1,0:T(8,128)(2,1)}), bf16[4,128,1024]{2,1,0:T(8,128)(2,1)}, u32[]{:S(2)}, u32[]{:S(2)}) async-start(bf16[4,128,1024]{2,1,0:T(8,128)(2,1)} %convert_element_type.558), calls=%async_computation.3 | async-start | bytes 2097152 | tf_op jit(solution)/shard_map/all_to_all | solution.py:187
  192.3 2.3 copy-start.1
  196.4 13.9 %copy-start.4 = (bf16[64,8,8,128]{3,2,1,0:T(8,128)(2,1)S(1)}, bf16[64,8,8,128]{3,2,1,0:T(8,128)(2,1)}, u32[]{:S(2)}) copy-start(bf16[64,8,8,128]{3,2,1,0:T(8,128)(2,1)} %copy-done.2) | copy-start | bytes 3145732
  206.8 17.9 %all-to-all-start.6 = ((bf16[4,128,1024]{1,2,0:T(8,128)(2,1)}), bf16[4,128,1024]{1,2,0:T(8,128)(2,1)S(1)}, u32[]{:S(2)}, u32[]{:S(2)}) async-start(bf16[4,128,1024]{1,2,0:T(8,128)(2,1)} %copy.130), calls=%async_computation.7 | async-start | bytes 2097152 | tf_op jit(solution)/shard_map/all_to_all | solution.py:190
  224.7 17.9 %all-to-all-start.5 = ((bf16[4,128,1024]{2,1,0:T(8,128)(2,1)}), bf16[4,128,1024]{2,1,0:T(8,128)(2,1)S(1)}, u32[]{:S(2)}, u32[]{:S(2)}) async-start(bf16[4,128,1024]{2,1,0:T(8,128)(2,1)} %all_to_all.103), calls=%async_computation.6 | async-start | bytes 2097152 | tf_op jit(solution)/shard_map/all_to_all | solution.py:189
Sparse Core Ops, SparseCore 0:
  55.0 102.2 reduce-scatter.1
